TPU v7x, 32 devices: a 4x4x1 block of a 4x4x8 slice. The times are simulated.
32 devices in a mesh: dp: 2 (over z, core), tp: 16 (over x, y).
Axes of the slice: x: 4, y: 4, z: 1, core: 2. Of those that a mesh axis runs over, the one named last changes fastest.
The devices are a block of a 4x4x8 slice.
Arguments:
- x: bfloat16 [128, 4096], P('dp'), parts along dimension 0
- k_cache: bfloat16 [128, 2048, 64, 64], P('dp', None, 'tp'), parts along dimension 0
- v_cache: bfloat16 [128, 2048, 64, 64], P('dp', None, 'tp'), parts along dimension 0
- gain_a: bfloat16 [4096], replicated
- wq: bfloat16 [4096, 4096], P(None, 'tp')
- wo: bfloat16 [4096, 4096], P('tp')
- gain_m: bfloat16 [4096], replicated
- w_gate: bfloat16 [4096, 10240], P(None, 'tp')
- w_up: bfloat16 [4096, 10240], P(None, 'tp')
- w_down: bfloat16 [10240, 4096], P('tp')
Outputs:
- output: bfloat16 [128, 4096], P('dp'), parts along dimension 0
There are 2 independent parts. A program takes and returns all parts, laid end to end along the dimension named above; an argument that names none is the same for every part.
All inputs are finite; a program needn't handle non-finite values.
Results may differ from a plain program's by a relative error of at most 0.017.
Values are sent between devices in bfloat16 or wider.
A program may use at most 768 MiB of HBM per device.

v0:
```python
import jax
import jax.numpy as jnp
from jax import lax
from jax.sharding import PartitionSpec as P

HEAD = 64
THETA = 10000


def normed(x, gain):
    wide = x.astype(jnp.float32)
    scale = lax.rsqrt(jnp.mean(wide * wide, -1, keepdims=True) + 1e-6)
    return (wide * scale * gain.astype(jnp.float32)).astype(jnp.bfloat16)


def turned(t, place, theta):
    half = t.shape[-1] // 2
    angle = place.astype(jnp.float32)[:, None] * theta ** (-jnp.arange(half, dtype=jnp.float32) / half)
    cos, sin = jnp.cos(angle)[:, None], jnp.sin(angle)[:, None]
    a, b = t[..., :half].astype(jnp.float32), t[..., half:].astype(jnp.float32)
    return jnp.concatenate([a * cos - b * sin, b * cos + a * sin], -1).astype(jnp.bfloat16)


def matmul(a, w):
    return jnp.dot(a, w, preferred_element_type=jnp.float32).astype(jnp.bfloat16)


def einsum(form, a, b):
    return jnp.einsum(form, a.astype(jnp.float32), b.astype(jnp.float32))


def seen_by(a, wq, k_cache, v_cache, head, theta):
    batch, cache, kv_heads = k_cache.shape[:3]
    place = jnp.full((batch,), cache - 1)
    q = turned(matmul(a, wq).reshape(batch, -1, head), place, theta).reshape(batch, kv_heads, -1, head)
    scores = einsum("bgsd,bugd->bgsu", q, k_cache) * head**-0.5
    weights = jax.nn.softmax(scores, -1).astype(jnp.bfloat16)
    return einsum("bgsu,bugd->bgsd", weights, v_cache).astype(jnp.bfloat16).reshape(batch, -1)


def hidden_of(b, w_gate, w_up):
    gate = jnp.dot(b, w_gate, preferred_element_type=jnp.float32)
    up = jnp.dot(b, w_up, preferred_element_type=jnp.float32)
    return (jax.nn.silu(gate) * up).astype(jnp.bfloat16)


def solution(mesh):
    def added(t, term):
        return (t.astype(jnp.float32) + lax.psum(term.astype(jnp.bfloat16), "tp").astype(jnp.float32)).astype(jnp.bfloat16)

    def step(x, k_cache, v_cache, gain_a, wq, wo, gain_m, w_gate, w_up, w_down):
        seen = seen_by(normed(x, gain_a), wq, k_cache, v_cache, HEAD, THETA)
        h = added(x, jnp.dot(seen, wo, preferred_element_type=jnp.float32))
        return added(h, jnp.dot(hidden_of(normed(h, gain_m), w_gate, w_up), w_down, preferred_element_type=jnp.float32))

    states, cache, columns, rows_of = P("dp", None), P("dp", None, "tp", None), P(None, "tp"), P("tp", None)
    return jax.shard_map(
        step,
        mesh=mesh,
        in_specs=(states, cache, cache, P(None), columns, rows_of, P(None), columns, columns, rows_of),
        out_specs=states,
        check_vma=False,
    )
```

profile of v0, /device:TPU:96, one launch (start us, length us, event | category | flops | bytes accessed | tf_op | source)
XLA Modules:
  0.0 239.8 jit_solution(10230221124982541541)
XLA Ops:
  6.5 0.0 copy-start
  6.6 0.0 all-reduce.3.cloned.1.call-start
  6.6 0.8 convert_element_type.66
  7.4 1.2 fusion.11
  8.7 2.3 convolution_convert_fusion.2
  11.0 0.1 copy.11
  11.1 0.1 fusion.34
  11.3 0.1 copy.12
  11.4 24.0 %fusion.45 = f32[64,4,1,2048]{3,2,1,0:T(1,128)} fusion(bf16[64,4,64,1]{2,3,1,0:T(2,128)(2,1)S(1)} %copy.12, bf16[64,2048,4,64]{1,3,2,0:T(8,128)(2,1)} %param.11), kind=kOutput, calls=%fused_computation.58 | convolution fusion | flops 67108864 | bytes 69238784 | tf_op jit(solution)/shard_map/bgsd,bugd->bgsu/dot_general | solution.py:29
  35.4 4.3 %fusion.6 = bf16[64,4,2048,1]{2,0,1,3:T(8,128)(2,1)S(1)} fusion(f32[64,4,1,2048]{3,2,1,0:T(1,128)} %fusion.45), kind=kOutput, calls=%fused_computation.8 | output fusion | flops 2101758 | bytes 3145728 | tf_op jit(solution)/shard_map/div | solution.py:37
  39.7 25.7 %fusion.7 = f32[64,4,1,64]{3,2,1,0:T(1,128)S(1)} fusion(bf16[64,2048,4,64]{1,3,2,0:T(8,128)(2,1)} %param.12, bf16[64,4,2048,1]{2,0,1,3:T(8,128)(2,1)S(1)} %fusion.6), kind=kOutput, calls=%fused_computation.10 | convolution fusion | flops 67108864 | bytes 68222976 | tf_op jit(solution)/shard_map/bgsu,bugd->bgsd/dot_general | solution.py:29
  65.4 0.0 copy-start.2
  65.4 0.0 copy-start.1
  65.5 0.1 reshape.62
  65.6 0.0 copy-done
  65.6 1.3 convolution_convert_fusion.1
  66.9 0.1 all-reduce.3.cloned.1.call-update
  66.9 0.1 all-reduce.5.cloned.1.call-start
  67.0 0.0 copy-done.2
  67.0 77.7 %all-reduce.3.cloned.1.call-done = bf16[64,4096]{1,0:T(8,128)(2,1)} async-done(((bf16[64,4096]{1,0:T(8,128)(2,1)}), bf16[64,4096]{1,0:T(8,128)(2,1)}) %all-reduce.3.cloned.1.call-update) | async-done | bytes 524304 | tf_op jit(solution)/shard_map/psum | solution.py:49
  144.7 0.0 copy-done.1
  144.7 1.3 fusion.15
  146.0 3.6 %fusion.30 = f32[64,640]{1,0:T(8,128)S(1)} fusion(bf16[4096,640]{1,0:T(8,128)(2,1)} %param.17, bf16[64,4096]{1,0:T(8,128)(2,1)S(1)} %get-tuple-element.6, f32[4096]{0:T(1024)S(1)} %convert_element_type.77, f32[64]{0:T(128)S(1)} %add_rsqrt_fusion), kind=kOutput, calls=%fused_computation.38 | convolution fusion | flops 336592896 | bytes 5947648 | tf_op jit(solution)/shard_map/dot_general | solution.py:42
  149.6 6.9 %convolution_convert_fusion = bf16[64,4096]{1,0:T(8,128)(2,1)} fusion(bf16[640,4096]{1,0:T(8,128)(2,1)} %param.19, bf16[4096,640]{1,0:T(8,128)(2,1)} %param.18, f32[64,640]{1,0:T(8,128)S(1)} %fusion.30, bf16[64,4096]{1,0:T(8,128)(2,1)S(1)} %get-tuple-element.6, f32[4096]{0:T(1024)S(1)} %convert_element_type.77, f32[64]{0:T(128)S(1)} %add_rsqrt_fusion), kind=kOutput, calls=%fused_computation.2 | convolution fusion | flops 672645120 | bytes 11714816 | tf_op jit(solution)/shard_map/dot_general | solution.py:54
  156.5 0.1 all-reduce.5.cloned.1.call-update
  156.5 74.5 %all-reduce.5.cloned.1.call-done = bf16[64,4096]{1,0:T(8,128)(2,1)} async-done(((bf16[64,4096]{1,0:T(8,128)(2,1)}), bf16[64,4096]{1,0:T(8,128)(2,1)}) %all-reduce.5.cloned.1.call-update) | async-done | bytes 524304 | tf_op jit(solution)/shard_map/psum | solution.py:49
  231.0 2.0 fusion.18
  (6 shorter events, 0.1 us)
Async XLA Ops:
  6.5 59.0 %copy-start = (bf16[256,4096]{1,0:T(8,128)(2,1)S(1)}, bf16[256,4096]{1,0:T(8,128)(2,1)}, u32[]{:S(2)}) copy-start(bf16[256,4096]{1,0:T(8,128)(2,1)} %param.15) | copy-start | bytes 6291460
  6.6 138.1 %all-reduce.3.cloned.1.call-start = ((), (), s32[]{:S(2)}) async-start(), calls=%async_computation | async-start | bytes 1048576 | tf_op jit(solution)/shard_map/psum | solution.py:49
  65.4 1.6 copy-start.2
  65.4 79.3 %copy-start.1 = (bf16[64,4096]{1,0:T(8,128)(2,1)S(1)}, bf16[64,4096]{1,0:T(8,128)(2,1)}, u32[]{:S(2)}) copy-start(bf16[64,4096]{1,0:T(8,128)(2,1)} %param.10) | copy-start | bytes 1572868
  66.9 164.1 %all-reduce.5.cloned.1.call-start = ((), (), s32[]{:S(2)}) async-start(), calls=%async_computation.1 | async-start | bytes 1048576 | tf_op jit(solution)/shard_map/psum | solution.py:49
Sparse Core Ops, SparseCore 0:
  67.0 77.5 all-reduce.2
  156.6 74.3 all-reduce.4
where the time goes:
time: 240 us
  waiting for transfers between devices  152 us (63%)
  matrix products  63.7 us (27%)
  between operations  13.5 us (6%)
  other arithmetic  9.86 us (4%)
    psum x2, waiting for transfers between devices, added(): lax.psum(term.astype(jnp.bfloat16), 'tp').astype(jnp.float32)  152 us
    dot_general x2, matrix products, einsum(): return jnp.einsum(form, a.astype(jnp.float32), b.astype(jnp.float32))  49.7 us
    dot_general x1, matrix products, step(): jnp.dot(hidden_of(normed(h, gain_m), w_gate, w_up), w_down, preferred_ele...  6.88 us
  transfers between devices with their start and end apart: 2, of which 2 were waited for; matrix products, arithmetic and copies ran while one was open for 0% of the time, Pallas kernels for 0%

commit v1 on v0

--- a/solution.py
+++ b/solution.py
@@ -1,6 +1,10 @@
+import functools
+
 import jax
 import jax.numpy as jnp
 from jax import lax
+from jax.experimental import pallas as pl
+from jax.experimental.pallas import tpu as pltpu
 from jax.sharding import PartitionSpec as P
 
 HEAD = 64
@@ -44,9 +48,70 @@
     return (jax.nn.silu(gate) * up).astype(jnp.bfloat16)
 
 
+def sum_kernel(n, t_ref, term_ref, out_ref, got, send_sem, recv_sem, send2_sem, recv2_sem):
+    me = lax.axis_index("tp")
+    rows, width = t_ref.shape
+    cols = width // n
+
+    def block(p):
+        return pl.ds(pl.multiple_of(p * cols, cols), cols)
+
+    barrier = pltpu.get_barrier_semaphore()
+    for k in range(1, n):
+        pl.semaphore_signal(barrier, inc=1, device_id={"tp": lax.rem(me + k, n)})
+    pl.semaphore_wait(barrier, n - 1)
+
+    sends = []
+    for k in range(1, n):
+        p = lax.rem(me + k, n)
+        copy = pltpu.make_async_remote_copy(
+            src_ref=term_ref.at[:, block(p)],
+            dst_ref=got.at[k - 1],
+            send_sem=send_sem.at[k - 1],
+            recv_sem=recv_sem.at[k - 1],
+            device_id={"tp": p},
+        )
+        copy.start()
+        sends.append(copy)
+    total = t_ref[:, block(me)].astype(jnp.float32) + term_ref[:, block(me)].astype(jnp.float32)
+    for k in range(1, n):
+        sends[k - 1].wait_recv()
+        total += got[k - 1].astype(jnp.float32)
+    out_ref[:, block(me)] = total.astype(jnp.bfloat16)
+    shares = []
+    for k in range(1, n):
+        p = lax.rem(me + k, n)
+        copy = pltpu.make_async_remote_copy(
+            src_ref=out_ref.at[:, block(me)],
+            dst_ref=out_ref.at[:, block(me)],
+            send_sem=send2_sem.at[k - 1],
+            recv_sem=recv2_sem.at[k - 1],
+            device_id={"tp": p},
+        )
+        copy.start()
+        shares.append(copy)
+    for copy in shares:
+        copy.wait_recv()
+    for copy in sends + shares:
+        copy.wait_send()
+
+
 def solution(mesh):
+    n = mesh.shape["tp"]
+
     def added(t, term):
-        return (t.astype(jnp.float32) + lax.psum(term.astype(jnp.bfloat16), "tp").astype(jnp.float32)).astype(jnp.bfloat16)
+        rows, width = t.shape
+        vmem = pl.BlockSpec(memory_space=pltpu.VMEM)
+        return pl.pallas_call(
+            functools.partial(sum_kernel, n),
+            out_shape=jax.ShapeDtypeStruct(t.shape, jnp.bfloat16),
+            in_specs=[vmem, vmem],
+            out_specs=vmem,
+            scratch_shapes=[pltpu.VMEM((n - 1, rows, width // n), jnp.bfloat16)]
+            + [pltpu.SemaphoreType.DMA((n - 1,))] * 4,
+            compiler_params=pltpu.CompilerParams(collective_id=0, has_side_effects=True),
+            name="added",
+        )(t, term.astype(jnp.bfloat16))
 
     def step(x, k_cache, v_cache, gain_a, wq, wo, gain_m, w_gate, w_up, w_down):
         seen = seen_by(normed(x, gain_a), wq, k_cache, v_cache, HEAD, THETA)

time: 240 us -> 124 us (0.52)
  waiting for transfers between devices: 152 us -> 0 us
  Pallas kernels: 0 us -> 49.7 us
  between operations: 13.5 us -> 0.15 us
    psum x2 -> x0, waiting for transfers between devices: 152 us -> none  [added(): lax.psum(term.astype(jnp.bfloat16), 'tp').astype(jnp.float32)]
    pallas_call x0 -> x2, Pallas kernels: none -> 49.7 us  [added(): pl.pallas_call(functools.partial(sum_kernel, n), out_shape=jax.ShapeDtype...]
  transfers between devices with their start and end apart: 2 -> 0, of which waited for: 2 -> 0; matrix products, arithmetic and copies ran while one was open for 0% -> 0% of each run, Pallas kernels for 0% -> 0%
where the time goes in v1:
time: 124 us
  matrix products  63.9 us (52%)
  Pallas kernels  49.7 us (40%)
  other arithmetic  7.82 us (6%)
  local copies, waits for them, and re-layouts  2.24 us (2%)
    dot_general x2, matrix products, einsum(): return jnp.einsum(form, a.astype(jnp.float32), b.astype(jnp.float32))  49.7 us
    pallas_call x2, Pallas kernels, added(): pl.pallas_call(functools.partial(sum_kernel, n), out_shape=jax.ShapeDtype...  49.7 us
    dot_general x1, matrix products, step(): jnp.dot(hidden_of(normed(h, gain_m), w_gate, w_up), w_down, preferred_ele...  6.87 us
    div x1, other arithmetic, seen_by(): weights = jax.nn.softmax(scores, -1).astype(jnp.bfloat16)  4.29 us
    dot_general x1, matrix products, hidden_of(): gate = jnp.dot(b, w_gate, preferred_element_type=jnp.float32)  3.76 us
    reduce_sum x2, other arithmetic, normed(): scale = lax.rsqrt(jnp.mean(wide * wide, -1, keepdims=True) + 1e-06)  2.49 us

profile of v1, /device:TPU:96, one launch (start us, length us, event | category | flops | bytes accessed | tf_op | source)
XLA Modules:
  0.0 123.8 jit_solution(2018340531366255939)
XLA Ops:
  0.0 0.0 copy-start
  0.1 0.8 convert_element_type.52
  0.9 1.2 %fusion.11 = f32[64]{0:T(128)S(1)} fusion(bf16[64,4096]{1,0:T(8,128)(2,1)} %t_ref.1), kind=kLoop, calls=%fused_computation.20 | loop fusion | flops 786368 | bytes 524544 | tf_op jit(solution)/shard_map/reduce_sum | solution.py:16
  2.2 2.3 %convolution_convert_fusion.2 = bf16[64,256]{1,0:T(8,128)(2,1)S(1)} fusion(bf16[4096,256]{1,0:T(8,128)(2,1)} %param.14, bf16[64,4096]{1,0:T(8,128)(2,1)} %t_ref.1, f32[4096]{0:T(1024)S(1)} %convert_element_type.52, f32[64]{0:T(128)S(1)} %add_rsqrt_fusion.1), kind=kOutput, calls=%fused_computation.19 | convolution fusion | flops 135282688 | bytes 2670848 | tf_op jit(solution)/shard_map/dot_general | solution.py:29
  4.5 0.1 copy.11
  4.6 0.1 fusion.32
  4.7 0.1 copy.12
  4.8 24.0 %fusion.42 = f32[64,4,1,2048]{3,2,1,0:T(1,128)} fusion(bf16[64,4,64,1]{2,3,1,0:T(2,128)(2,1)S(1)} %copy.12, bf16[64,2048,4,64]{1,3,2,0:T(8,128)(2,1)} %param.11), kind=kOutput, calls=%fused_computation.54 | convolution fusion | flops 67108864 | bytes 69238784 | tf_op jit(solution)/shard_map/bgsd,bugd->bgsu/dot_general | solution.py:33
  28.8 4.3 %fusion.6 = bf16[64,4,2048,1]{2,0,1,3:T(8,128)(2,1)S(1)} fusion(f32[64,4,1,2048]{3,2,1,0:T(1,128)} %fusion.42), kind=kOutput, calls=%fused_computation.8 | output fusion | flops 2101758 | bytes 3145728 | tf_op jit(solution)/shard_map/div | solution.py:41
  33.1 25.7 %fusion.7 = f32[64,4,1,64]{3,2,1,0:T(1,128)S(1)} fusion(bf16[64,2048,4,64]{1,3,2,0:T(8,128)(2,1)} %param.12, bf16[64,4,2048,1]{2,0,1,3:T(8,128)(2,1)S(1)} %fusion.6), kind=kOutput, calls=%fused_computation.10 | convolution fusion | flops 67108864 | bytes 68222976 | tf_op jit(solution)/shard_map/bgsu,bugd->bgsd/dot_general | solution.py:33
  58.9 0.1 reshape.62
  59.0 0.0 copy-done
  59.0 0.0 copy-start.2
  59.0 1.3 %convolution_convert_fusion.1.term_ref = bf16[64,4096]{1,0:T(8,128)(2,1)} fusion(bf16[64,256]{1,0:T(8,128)(2,1)S(1)} %reshape.62, bf16[256,4096]{1,0:T(8,128)(2,1)S(1)} %copy-done), kind=kOutput, calls=%fused_computation.3 | convolution fusion | flops 134479872 | bytes 2654208 | tf_op jit(solution)/shard_map/dot_general | solution.py:118
  60.3 27.4 %added.2.t_ref = bf16[64,4096]{1,0:T(8,128)(2,1)} custom-call(bf16[64,4096]{1,0:T(8,128)(2,1)} %t_ref.1, bf16[64,4096]{1,0:T(8,128)(2,1)} %convolution_convert_fusion.1.term_ref), custom_call_target="tpu_custom_call" | custom-call | tf_op jit(solution)/shard_map/added/pallas_call | solution.py:105
  87.7 1.2 %fusion.14 = f32[64]{0:T(128)S(1)} fusion(bf16[64,4096]{1,0:T(8,128)(2,1)} %added.2.t_ref), kind=kLoop, calls=%fused_computation.23 | loop fusion | flops 786368 | bytes 524544 | tf_op jit(solution)/shard_map/reduce_sum | solution.py:16
  89.0 0.0 copy-done.2
  89.0 0.0 copy-start.1
  89.0 3.8 %fusion.28 = f32[64,640]{1,0:T(8,128)S(1)} fusion(bf16[4096,640]{1,0:T(8,128)(2,1)} %param.17, bf16[64,4096]{1,0:T(8,128)(2,1)} %added.2.t_ref, f32[4096]{0:T(1024)S(1)} %convert_element_type.61, f32[64]{0:T(128)S(1)} %add_rsqrt_fusion), kind=kOutput, calls=%fused_computation.34 | convolution fusion | flops 336592896 | bytes 5947648 | tf_op jit(solution)/shard_map/dot_general | solution.py:46
  92.8 0.0 copy-done.1
  92.8 6.9 %convolution_convert_fusion.term_ref = bf16[64,4096]{1,0:T(8,128)(2,1)} fusion(bf16[640,4096]{1,0:T(8,128)(2,1)} %param.19, bf16[4096,640]{1,0:T(8,128)(2,1)} %param.18, f32[64,640]{1,0:T(8,128)S(1)} %fusion.28, bf16[64,4096]{1,0:T(8,128)(2,1)S(1)} %copy-done.1, f32[4096]{0:T(1024)S(1)} %convert_element_type.61, f32[64]{0:T(128)S(1)} %add_rsqrt_fusion), kind=kOutput, calls=%fused_computation.2 | convolution fusion | flops 672645120 | bytes 11714816 | tf_op jit(solution)/shard_map/dot_general | solution.py:119
  99.7 22.2 %added.3 = bf16[64,4096]{1,0:T(8,128)(2,1)} custom-call(bf16[64,4096]{1,0:T(8,128)(2,1)} %added.2.t_ref, bf16[64,4096]{1,0:T(8,128)(2,1)} %convolution_convert_fusion.term_ref), custom_call_target="tpu_custom_call" | custom-call | tf_op jit(solution)/shard_map/added/pallas_call | solution.py:105
  121.9 1.9 %copy.25 = bf16[64,4096]{1,0:T(8,128)(2,1)} copy(bf16[64,4096]{1,0:T(8,128)(2,1)} %added.3) | data formatting | bytes 1048576
  (6 shorter events, 0.1 us)
Async XLA Ops:
  0.0 59.0 %copy-start = (bf16[256,4096]{1,0:T(8,128)(2,1)S(1)}, bf16[256,4096]{1,0:T(8,128)(2,1)}, u32[]{:S(2)}) copy-start(bf16[256,4096]{1,0:T(8,128)(2,1)} %param.15) | copy-start | bytes 6291460
  59.0 30.0 %copy-start.2 = (bf16[4096]{0:T(1024)(128)(2,1)S(1)}, bf16[4096]{0:T(1024)(128)(2,1)}, u32[]{:S(2)}) copy-start(bf16[4096]{0:T(1024)(128)(2,1)} %param.16) | copy-start | bytes 24580
  89.0 3.8 %copy-start.1 = (bf16[64,4096]{1,0:T(8,128)(2,1)S(1)}, bf16[64,4096]{1,0:T(8,128)(2,1)}, u32[]{:S(2)}) copy-start(bf16[64,4096]{1,0:T(8,128)(2,1)} %added.2.t_ref) | copy-start | bytes 1572868

commit v2 on v0

v2 whole, which is shorter than its diff:
```python
import functools

import jax
import jax.numpy as jnp
import numpy as np
from jax import lax
from jax.experimental import pallas as pl
from jax.experimental.pallas import tpu as pltpu
from jax.sharding import PartitionSpec as P

HEAD = 64
THETA = 10000
GROUP = 4
CHUNK = 16
SLOTS = 3

F32, BF16 = jnp.float32, jnp.bfloat16


def iota(shape, axis):
    return lax.broadcasted_iota(jnp.int32, shape, axis)


def layer_kernel(n, dims, x_hbm, k_hbm, v_hbm, gain_a, wq_hbm, wo_hbm, gain_m, wg_hbm, wu_hbm, wd_hbm, turn, out,
                 x, a, wq, wo, wgu, wd, kbuf, vbuf, qx, seen, term, h, got, term2, got2,
                 in_sem, k_sem, v_sem, send_sem, rs_sem, ag_sem, rs2_sem, ag2_sem):
    batch, width, heads, cache, hidden = dims
    mine = heads * HEAD
    cols = width // n
    chunks, groups = batch // CHUNK, batch // GROUP
    per = groups // chunks
    me = lax.axis_index("tp")

    def block(p):
        return pl.ds(pl.multiple_of(p * cols, cols), cols)

    def rows(c):
        return pl.ds(pl.multiple_of(c * CHUNK, CHUNK), CHUNK)

    def peer(k):
        return lax.rem(me + k, n)

    def take(i, src, dst):
        return pltpu.make_async_copy(src, dst, in_sem.at[i])

    take_x, take_wq, take_wo = take(0, x_hbm, x), take(1, wq_hbm, wq), take(2, wo_hbm, wo)
    take_wg = take(3, wg_hbm, wgu.at[:, pl.ds(0, hidden)])
    take_wu = take(4, wu_hbm, wgu.at[:, pl.ds(hidden, hidden)])
    take_wd = take(5, wd_hbm, wd)

    def take_k(g):
        s = lax.rem(g, SLOTS)
        return pltpu.make_async_copy(k_hbm.at[pl.ds(g * GROUP, GROUP)], kbuf.at[s], k_sem.at[s])

    def take_v(g):
        s = lax.rem(g, SLOTS)
        return pltpu.make_async_copy(v_hbm.at[pl.ds(g * GROUP, GROUP)], vbuf.at[s], v_sem.at[s])

    take_x.start()
    take_wq.start()
    for g in range(SLOTS):
        take_k(g).start()
        take_v(g).start()
        if g == 0:
            take_wo.start()

    barrier = pltpu.get_barrier_semaphore()
    for k in range(1, n):
        pl.semaphore_signal(barrier, inc=1, device_id={"tp": peer(k)})

    def all_arrived(sem):
        pltpu.make_async_copy(got.at[0], got.at[0], sem).wait()

    def scatter(c, src, dst, sem):
        for k in range(1, n):
            pltpu.make_async_remote_copy(
                src_ref=src.at[rows(c), block(peer(k))],
                dst_ref=dst.at[c, k - 1],
                send_sem=send_sem,
                recv_sem=sem.at[c],
                device_id={"tp": peer(k)},
            ).start()

    def share(c, ref, sem):
        for k in range(1, n):
            pltpu.make_async_remote_copy(
                src_ref=ref.at[rows(c), block(me)],
                dst_ref=ref.at[rows(c), block(me)],
                send_sem=send_sem,
                recv_sem=sem.at[c],
                device_id={"tp": peer(k)},
            ).start()

    def finish(c, base, own, came, dst):
        total = base[rows(c), block(me)].astype(F32) + own[rows(c), block(me)].astype(F32)
        for k in range(n - 1):
            total += came[c, k].astype(F32)
        dst[rows(c), block(me)] = total.astype(BF16)

    def norm(c, src, gain, dst):
        wide = src[rows(c), :].astype(F32)
        scale = lax.rsqrt(jnp.mean(wide * wide, -1, keepdims=True) + 1e-6)
        dst[rows(c), :] = (wide * scale * gain[...].astype(F32)).astype(BF16)

    def each(count, body):
        lax.fori_loop(0, count, lambda i, _: (body(i), None)[1], None)

    take_x.wait()
    each(chunks, lambda c: norm(c, x, gain_a, a))
    take_wq.wait()
    q = jnp.dot(a[...], wq[...], preferred_element_type=F32).astype(BF16).astype(F32)
    low = lax.rem(iota(q.shape, 1), HEAD) < HEAD // 2
    other = jnp.where(low, pltpu.roll(q, mine - HEAD // 2, 1), pltpu.roll(q, HEAD // 2, 1))
    q = (q * turn[0:1, :] + other * turn[1:2, :]).astype(BF16)
    spread = (iota((batch * heads, batch), 0) // heads == iota((batch * heads, batch), 1)).astype(BF16)
    wide_q = jnp.dot(spread, q, preferred_element_type=F32)
    own_head = iota(wide_q.shape, 1) // HEAD == lax.rem(iota(wide_q.shape, 0), heads)
    qx[...] = jnp.where(own_head, wide_q, 0.0).astype(BF16)

    size = GROUP * heads
    row_of = iota((size, mine), 0)
    of_head = iota((size, mine), 1) // HEAD == lax.rem(row_of, heads)
    gather = (iota((CHUNK, CHUNK * heads), 1) // heads == iota((CHUNK, CHUNK * heads), 0)).astype(BF16)

    def attend(g, at):
        s = lax.rem(g, SLOTS)
        q16 = qx[pl.ds(pl.multiple_of(g * size, size), size), :].astype(F32)
        lhs = jnp.concatenate([jnp.where(row_of // heads == b, q16, 0.0).astype(BF16) for b in range(GROUP)], 1)
        take_k(g).wait()
        scores = jnp.dot(lhs, kbuf[s].reshape(GROUP * mine, cache), preferred_element_type=F32) * HEAD**-0.5
        e = jnp.exp(scores - jnp.max(scores, -1, keepdims=True))
        weights = (e * (1.0 / jnp.sum(e, -1, keepdims=True))).astype(BF16)
        take_v(g).wait()
        result = jnp.zeros((size, mine), F32)
        for b in range(GROUP):
            part = lax.dot_general(weights, vbuf[s, b], (((1,), (1,)), ((), ())), preferred_element_type=F32)
            result = jnp.where(row_of // heads == b, part, result)
        seen[pl.ds(pl.multiple_of(at * size, size), size), :] = jnp.where(of_head, result, 0.0).astype(BF16)

        @pl.when(g + SLOTS < groups)
        def _():
            take_k(g + SLOTS).start()
            take_v(g + SLOTS).start()

        for i, copy in enumerate((take_wg, take_wu, take_wd)):
            pl.when(g == groups - SLOTS + i)(copy.start)

    def reduce(c):
        all_arrived(rs_sem.at[c])
        finish(c, x, term, got, h)
        share(c, h, ag_sem)

    def chunk(c):
        each(per, lambda i: attend(c * per + i, i))
        now = jnp.dot(gather, seen[...], preferred_element_type=F32).astype(BF16)

        @pl.when(c == 0)
        def _():
            take_wo.wait()
            pl.semaphore_wait(barrier, n - 1)

        term[rows(c), :] = jnp.dot(now, wo[...], preferred_element_type=F32).astype(BF16)
        scatter(c, term, got, rs_sem)
        pl.when(c > 0)(lambda: reduce(c - 1))

    each(chunks, chunk)
    reduce(chunks - 1)

    def normed_again(c):
        all_arrived(ag_sem.at[c])
        norm(c, h, gain_m, a)

    each(chunks, normed_again)
    take_wg.wait()
    take_wu.wait()
    both = jnp.dot(a[...], wgu[...], preferred_element_type=F32)
    inner = (jax.nn.silu(both[:, :hidden]) * both[:, hidden:]).astype(BF16)
    take_wd.wait()
    term2[...] = jnp.dot(inner, wd[...], preferred_element_type=F32).astype(BF16)
    each(chunks, lambda c: scatter(c, term2, got2, rs2_sem))

    def reduce2(c):
        all_arrived(rs2_sem.at[c])
        finish(c, h, term2, got2, out)
        share(c, out, ag2_sem)

    each(chunks, reduce2)
    each(chunks, lambda c: all_arrived(ag2_sem.at[c]))
    each(4 * chunks, lambda c: all_arrived(send_sem))


def turns(place, heads):
    half = HEAD // 2
    angle = np.float32(place) * np.float32(THETA) ** (-np.arange(half, dtype=np.float32) / np.float32(half))
    cos, sin = np.cos(angle), np.sin(angle)
    return np.stack([np.tile(cos, 2 * heads), np.tile(np.concatenate([-sin, sin]), heads)]).astype(np.float32)


def solution(mesh):
    n = mesh.shape["tp"]

    def step(x, k_cache, v_cache, gain_a, wq, wo, gain_m, w_gate, w_up, w_down):
        batch, width = x.shape
        cache, heads = k_cache.shape[1:3]
        hidden = w_gate.shape[1]
        mine = heads * HEAD
        dims = batch, width, heads, cache, hidden

        def tall(t):
            return t.transpose(0, 2, 3, 1).reshape(batch, mine, cache)

        chunks = batch // CHUNK
        hbm, vmem = pl.BlockSpec(memory_space=pl.ANY), pl.BlockSpec(memory_space=pltpu.VMEM)
        got = pltpu.VMEM((chunks, n - 1, CHUNK, width // n), BF16)
        states = pltpu.VMEM((batch, width), BF16)
        dma = pltpu.SemaphoreType.DMA
        return pl.pallas_call(
            functools.partial(layer_kernel, n, dims),
            out_shape=jax.ShapeDtypeStruct(x.shape, BF16),
            in_specs=[hbm, hbm, hbm, vmem, hbm, hbm, vmem, hbm, hbm, hbm, vmem],
            out_specs=vmem,
            scratch_shapes=[
                states, states, pltpu.VMEM((width, mine), BF16), pltpu.VMEM((mine, width), BF16),
                pltpu.VMEM((width, 2 * hidden), BF16), pltpu.VMEM((hidden, width), BF16),
                pltpu.VMEM((SLOTS, GROUP, mine, cache), BF16), pltpu.VMEM((SLOTS, GROUP, mine, cache), BF16),
                pltpu.VMEM((batch * heads, mine), BF16), pltpu.VMEM((CHUNK * heads, mine), BF16),
                states, states, got, states, got,
                dma((6,)), dma((SLOTS,)), dma((SLOTS,)), dma, dma((chunks,)), dma((chunks,)), dma((chunks,)), dma((chunks,)),
            ],
            compiler_params=pltpu.CompilerParams(collective_id=0, has_side_effects=True, vmem_limit_bytes=63 * 2**20),
            name="layer",
        )(x, tall(k_cache), tall(v_cache), gain_a[None], wq, wo, gain_m[None], w_gate, w_up, w_down, turns(cache - 1, heads))

    states, cache, columns, rows_of = P("dp", None), P("dp", None, "tp", None), P(None, "tp"), P("tp", None)
    return jax.shard_map(
        step,
        mesh=mesh,
        in_specs=(states, cache, cache, P(None), columns, rows_of, P(None), columns, columns, rows_of),
        out_specs=states,
        check_vma=False,
    )
```

time: 240 us -> 81.4 us (0.34)
  waiting for transfers between devices: 152 us -> 0 us
  Pallas kernels: 0 us -> 76.6 us
  matrix products: 63.7 us -> 0 us
  between operations: 13.5 us -> 0.01 us
  other arithmetic: 9.86 us -> 0 us
  local copies, waits for them, and re-layouts: 0.37 us -> 4.48 us
    psum x2 -> x0, waiting for transfers between devices: 152 us -> none  [added(): lax.psum(term.astype(jnp.bfloat16), 'tp').astype(jnp.float32)]
    pallas_call x0 -> x1, Pallas kernels: none -> 76.6 us  [step(): pl.pallas_call(functools.partial(layer_kernel, n, dims), out_shape=jax.Sh...]
    dot_general x6 -> x0, matrix products: 63.7 us -> none  [the longest x2 49.7 us: einsum(): return jnp.einsum(form, a.astype(jnp.float32), b.astype(jnp.float32))]
    div x1 -> x0, other arithmetic: 4.29 us -> none  [seen_by(): weights = jax.nn.softmax(scores, -1).astype(jnp.bfloat16)]
    convert_element_type x4 -> x0, other arithmetic: 2.83 us -> none  [the longest x1 1.96 us: added(): (t.astype(jnp.float32) + lax.psum(term.astype(jnp.bfloat16), 'tp').astype...]
    broadcast_in_dim x0 -> x2, local copies, waits for them, and re-layouts: none -> 2.61 us  [the longest x1 1.31 us: step(): gain_a[None]]
    reduce_sum x2 -> x0, other arithmetic: 2.57 us -> none  [normed(): scale = lax.rsqrt(jnp.mean(wide * wide, -1, keepdims=True) + 1e-06)]
  transfers between devices with their start and end apart: 2 -> 0, of which waited for: 2 -> 0; matrix products, arithmetic and copies ran while one was open for 0% -> 0% of each run, Pallas kernels for 0% -> 0%
where the time goes in v2:
time: 81.4 us; the launch traced here: 81.1 us
  Pallas kernels  76.6 us (94%)
  local copies, waits for them, and re-layouts  4.48 us (6%)
    pallas_call x1, Pallas kernels, step(): pl.pallas_call(functools.partial(layer_kernel, n, dims), out_shape=jax.Sh...  76.6 us
    unnamed x1, local copies, waits for them, and re-layouts  1.87 us

profile of v2, /device:TPU:96, one launch (start us, length us, event | category | flops | bytes accessed | tf_op | source)
XLA Modules:
  0.0 81.1 jit_solution(12661286567486801101)
XLA Ops:
  0.0 1.3 %broadcast_in_dim.6.gain_a = bf16[1,4096]{1,0:T(2,128)(2,1)} reshape(bf16[4096]{0:T(1024)(128)(2,1)} %param.14) | data formatting | bytes 16384 | tf_op jit(solution)/shard_map/broadcast_in_dim | solution.py:232
  1.3 1.3 %broadcast_in_dim.7.gain_m = bf16[1,4096]{1,0:T(2,128)(2,1)} reshape(bf16[4096]{0:T(1024)(128)(2,1)} %param.17) | data formatting | bytes 16384 | tf_op jit(solution)/shard_map/broadcast_in_dim | solution.py:232
  2.6 76.6 %layer.1 = bf16[64,4096]{1,0:T(8,128)(2,1)} custom-call(bf16[64,4096]{1,0:T(8,128)(2,1)} %x_hbm.1, bf16[64,256,2048]{2,1,0:T(8,128)(2,1)} %bitcast.1.k_hbm, bf16[64,256,2048]{2,1,0:T(8,128)(2,1)} %bitcast.3.v_hbm, bf16[1,4096]{1,0:T(2,128)(2,1)} %broadcast_in_dim.6.gain_a, bf16[4096,256]{1,0:T(8,128)(2,1)} %wq_hbm.1, bf16[256,4096]{1,0:T(8,128)(2,1)} %wo_hbm.1, ...), custom_call_target="tpu_custom_call" | custom-call | tf_op jit(solution)/shard_map/layer/pallas_call | solution.py:217
  79.3 1.9 %copy.13 = bf16[64,4096]{1,0:T(8,128)(2,1)} copy(bf16[64,4096]{1,0:T(8,128)(2,1)} %layer.1) | data formatting | bytes 1048576

commit v3 on v2

--- a/solution.py
+++ b/solution.py
@@ -1,4 +1,5 @@
 import functools
+import math
 
 import jax
 import jax.numpy as jnp
@@ -21,8 +22,8 @@
     return lax.broadcasted_iota(jnp.int32, shape, axis)
 
 
-def layer_kernel(n, dims, x_hbm, k_hbm, v_hbm, gain_a, wq_hbm, wo_hbm, gain_m, wg_hbm, wu_hbm, wd_hbm, turn, out,
-                 x, a, wq, wo, wgu, wd, kbuf, vbuf, qx, seen, term, h, got, term2, got2,
+def layer_kernel(n, dims, x_hbm, k_hbm, v_hbm, ga_hbm, wq_hbm, wo_hbm, gm_hbm, wg_hbm, wu_hbm, wd_hbm, turn_hbm, out,
+                 x, a, gain1, gain2, gains, turn, wq, wo, wgu, wd, kbuf, vbuf, weights, qx, seen, term, h, got, inner, term2, got2,
                  in_sem, k_sem, v_sem, send_sem, rs_sem, ag_sem, rs2_sem, ag2_sem):
     batch, width, heads, cache, hidden = dims
     mine = heads * HEAD
@@ -37,8 +38,14 @@
     def rows(c):
         return pl.ds(pl.multiple_of(c * CHUNK, CHUNK), CHUNK)
 
+    side = math.isqrt(n)
+    shape = (side, side) if side * side == n else (1, n)
+    offsets = [(i, j) for i in range(shape[0]) for j in range(shape[1]) if i or j]
+    offsets.sort(key=lambda o: -min(o[0], shape[0] - o[0]) - min(o[1], shape[1] - o[1]))
+
     def peer(k):
-        return lax.rem(me + k, n)
+        i, j = offsets[k - 1]
+        return lax.rem(me // shape[1] + i, shape[0]) * shape[1] + lax.rem(me + j, shape[1])
 
     def take(i, src, dst):
         return pltpu.make_async_copy(src, dst, in_sem.at[i])
@@ -47,20 +54,29 @@
     take_wg = take(3, wg_hbm, wgu.at[:, pl.ds(0, hidden)])
     take_wu = take(4, wu_hbm, wgu.at[:, pl.ds(hidden, hidden)])
     take_wd = take(5, wd_hbm, wd)
+    small = take(6, ga_hbm, gain1), take(7, gm_hbm, gain2), take(8, turn_hbm, turn)
 
     def take_k(g):
         s = lax.rem(g, SLOTS)
         return pltpu.make_async_copy(k_hbm.at[pl.ds(g * GROUP, GROUP)], kbuf.at[s], k_sem.at[s])
 
-    def take_v(g):
+    def take_v(g, b):
         s = lax.rem(g, SLOTS)
-        return pltpu.make_async_copy(v_hbm.at[pl.ds(g * GROUP, GROUP)], vbuf.at[s], v_sem.at[s])
+        return pltpu.make_async_copy(v_hbm.at[g * GROUP + b], vbuf.at[s, b], v_sem.at[s, b])
+
+    def start_v(g):
+        for b in range(GROUP):
+            take_v(g, b).start()
 
     take_x.start()
+    for copy in small:
+        copy.start()
     take_wq.start()
+    take_k(0).start()
     for g in range(SLOTS):
-        take_k(g).start()
-        take_v(g).start()
+        if g + 1 < SLOTS:
+            take_k(g + 1).start()
+        start_v(g)
         if g == 0:
             take_wo.start()
 
@@ -97,16 +113,20 @@
             total += came[c, k].astype(F32)
         dst[rows(c), block(me)] = total.astype(BF16)
 
-    def norm(c, src, gain, dst):
+    def norm(c, src, i, dst):
         wide = src[rows(c), :].astype(F32)
         scale = lax.rsqrt(jnp.mean(wide * wide, -1, keepdims=True) + 1e-6)
-        dst[rows(c), :] = (wide * scale * gain[...].astype(F32)).astype(BF16)
+        dst[rows(c), :] = (wide * scale * gains[i : i + 1, :]).astype(BF16)
 
     def each(count, body):
         lax.fori_loop(0, count, lambda i, _: (body(i), None)[1], None)
 
+    for copy in small:
+        copy.wait()
+    for i, gain in enumerate((gain1, gain2)):
+        gains[i : i + 1, :] = gain[...].astype(F32).reshape(1, width)
     take_x.wait()
-    each(chunks, lambda c: norm(c, x, gain_a, a))
+    each(chunks, lambda c: norm(c, x, 0, a))
     take_wq.wait()
     q = jnp.dot(a[...], wq[...], preferred_element_type=F32).astype(BF16).astype(F32)
     low = lax.rem(iota(q.shape, 1), HEAD) < HEAD // 2
@@ -122,62 +142,90 @@
     of_head = iota((size, mine), 1) // HEAD == lax.rem(row_of, heads)
     gather = (iota((CHUNK, CHUNK * heads), 1) // heads == iota((CHUNK, CHUNK * heads), 0)).astype(BF16)
 
-    def attend(g, at):
-        s = lax.rem(g, SLOTS)
+    def weigh(g):
         q16 = qx[pl.ds(pl.multiple_of(g * size, size), size), :].astype(F32)
         lhs = jnp.concatenate([jnp.where(row_of // heads == b, q16, 0.0).astype(BF16) for b in range(GROUP)], 1)
-        take_k(g).wait()
-        scores = jnp.dot(lhs, kbuf[s].reshape(GROUP * mine, cache), preferred_element_type=F32) * HEAD**-0.5
+        keys = kbuf[lax.rem(g, SLOTS)].reshape(GROUP * mine, cache)
+        scores = jnp.dot(lhs, keys, preferred_element_type=F32) * HEAD**-0.5
         e = jnp.exp(scores - jnp.max(scores, -1, keepdims=True))
-        weights = (e * (1.0 / jnp.sum(e, -1, keepdims=True))).astype(BF16)
-        take_v(g).wait()
+        return (e * (1.0 / jnp.sum(e, -1, keepdims=True))).astype(BF16)
+
+    def value(g, b, result):
+        part = lax.dot_general(weights[...], vbuf[lax.rem(g, SLOTS), b], (((1,), (1,)), ((), ())), preferred_element_type=F32)
+        return jnp.where(row_of // heads == b, part, result)
+
+    def keep(g, result):
+        at = pl.ds(pl.multiple_of(lax.rem(g, per) * size, size), size)
+        seen[at, :] = jnp.where(of_head, result, 0.0).astype(BF16)
+
+    def attend(g):
+        take_k(g + 1).wait()
+        for b in range(GROUP):
+            take_v(g, b).wait()
         result = jnp.zeros((size, mine), F32)
         for b in range(GROUP):
-            part = lax.dot_general(weights, vbuf[s, b], (((1,), (1,)), ((), ())), preferred_element_type=F32)
-            result = jnp.where(row_of // heads == b, part, result)
-        seen[pl.ds(pl.multiple_of(at * size, size), size), :] = jnp.where(of_head, result, 0.0).astype(BF16)
-
-        @pl.when(g + SLOTS < groups)
-        def _():
-            take_k(g + SLOTS).start()
-            take_v(g + SLOTS).start()
-
+            result = value(g, b, result)
+        later = weigh(g + 1)
+        keep(g, result)
+        weights[...] = later
+        pl.when(g + 1 + SLOTS < groups)(lambda: take_k(g + 1 + SLOTS).start())
+        pl.when(g + SLOTS < groups)(lambda: start_v(g + SLOTS))
         for i, copy in enumerate((take_wg, take_wu, take_wd)):
-            pl.when(g == groups - SLOTS + i)(copy.start)
+            pl.when(g == groups - SLOTS + min(i, SLOTS - 2))(copy.start)
 
     def reduce(c):
         all_arrived(rs_sem.at[c])
         finish(c, x, term, got, h)
         share(c, h, ag_sem)
 
-    def chunk(c):
-        each(per, lambda i: attend(c * per + i, i))
+    def send(c):
         now = jnp.dot(gather, seen[...], preferred_element_type=F32).astype(BF16)
-
-        @pl.when(c == 0)
-        def _():
-            take_wo.wait()
-            pl.semaphore_wait(barrier, n - 1)
-
         term[rows(c), :] = jnp.dot(now, wo[...], preferred_element_type=F32).astype(BF16)
         scatter(c, term, got, rs_sem)
-        pl.when(c > 0)(lambda: reduce(c - 1))
-
-    each(chunks, chunk)
-    reduce(chunks - 1)
+
+    def step(g):
+        c, i = g // per, lax.rem(g, per)
+        pl.when((i == per // 2) & (c == 0))(lambda: pl.semaphore_wait(barrier, n - 1))
+        pl.when((i == per // 2) & (c > 0))(lambda: reduce(c - 1))
+        attend(g)
+        pl.when(g == 0)(take_wo.wait)
+        pl.when(i == per - 1)(lambda: send(c))
 
     def normed_again(c):
         all_arrived(ag_sem.at[c])
-        norm(c, h, gain_m, a)
-
-    each(chunks, normed_again)
+        norm(c, h, 1, a)
+
+    def up(r):
+        both = jnp.dot(a[r, :], wgu[...], preferred_element_type=F32)
+        inner[r, :] = (jax.nn.silu(both[:, :hidden]) * both[:, hidden:]).astype(BF16)
+
+    def down(r):
+        term2[r, :] = jnp.dot(inner[r, :], wd[...], preferred_element_type=F32).astype(BF16)
+
+    last = chunks - 1
+    take_k(0).wait()
+    weights[...] = weigh(0)
+    take_k(SLOTS).start()
+    each(groups - 1, step)
+    result = jnp.zeros((size, mine), F32)
+    for b in range(GROUP):
+        take_v(groups - 1, b).wait()
+        result = value(groups - 1, b, result)
+    keep(groups - 1, result)
+    send(last)
+    early, late = slice(0, last * CHUNK), slice(last * CHUNK, batch)
+    each(last, normed_again)
     take_wg.wait()
     take_wu.wait()
-    both = jnp.dot(a[...], wgu[...], preferred_element_type=F32)
-    inner = (jax.nn.silu(both[:, :hidden]) * both[:, hidden:]).astype(BF16)
+    up(early)
+    reduce(last)
     take_wd.wait()
-    term2[...] = jnp.dot(inner, wd[...], preferred_element_type=F32).astype(BF16)
-    each(chunks, lambda c: scatter(c, term2, got2, rs2_sem))
+    down(early)
+    each(last, lambda c: scatter(c, term2, got2, rs2_sem))
+    normed_again(last)
+    up(late)
+    down(late)
+    scatter(last, term2, got2, rs2_sem)
 
     def reduce2(c):
         all_arrived(rs2_sem.at[c])
@@ -210,26 +258,27 @@
             return t.transpose(0, 2, 3, 1).reshape(batch, mine, cache)
 
         chunks = batch // CHUNK
-        hbm, vmem = pl.BlockSpec(memory_space=pl.ANY), pl.BlockSpec(memory_space=pltpu.VMEM)
+        hbm, vmem = pl.BlockSpec(memory_space=pltpu.HBM), pl.BlockSpec(memory_space=pltpu.VMEM)
         got = pltpu.VMEM((chunks, n - 1, CHUNK, width // n), BF16)
         states = pltpu.VMEM((batch, width), BF16)
         dma = pltpu.SemaphoreType.DMA
         return pl.pallas_call(
             functools.partial(layer_kernel, n, dims),
-            out_shape=jax.ShapeDtypeStruct(x.shape, BF16),
-            in_specs=[hbm, hbm, hbm, vmem, hbm, hbm, vmem, hbm, hbm, hbm, vmem],
+            out_shape=pltpu.VMEM(x.shape, BF16),
+            in_specs=[hbm] * 11,
             out_specs=vmem,
             scratch_shapes=[
-                states, states, pltpu.VMEM((width, mine), BF16), pltpu.VMEM((mine, width), BF16),
+                states, states, pltpu.VMEM((width,), BF16), pltpu.VMEM((width,), BF16), pltpu.VMEM((2, width), F32), pltpu.VMEM((2, mine), F32),
+                pltpu.VMEM((width, mine), BF16), pltpu.VMEM((mine, width), BF16),
                 pltpu.VMEM((width, 2 * hidden), BF16), pltpu.VMEM((hidden, width), BF16),
                 pltpu.VMEM((SLOTS, GROUP, mine, cache), BF16), pltpu.VMEM((SLOTS, GROUP, mine, cache), BF16),
-                pltpu.VMEM((batch * heads, mine), BF16), pltpu.VMEM((CHUNK * heads, mine), BF16),
-                states, states, got, states, got,
-                dma((6,)), dma((SLOTS,)), dma((SLOTS,)), dma, dma((chunks,)), dma((chunks,)), dma((chunks,)), dma((chunks,)),
+                pltpu.VMEM((GROUP * heads, cache), BF16), pltpu.VMEM((batch * heads, mine), BF16), pltpu.VMEM((CHUNK * heads, mine), BF16),
+                states, states, got, pltpu.VMEM((batch, hidden), BF16), states, got,
+                dma((9,)), dma((SLOTS,)), dma((SLOTS, GROUP)), dma, dma((chunks,)), dma((chunks,)), dma((chunks,)), dma((chunks,)),
             ],
             compiler_params=pltpu.CompilerParams(collective_id=0, has_side_effects=True, vmem_limit_bytes=63 * 2**20),
             name="layer",
-        )(x, tall(k_cache), tall(v_cache), gain_a[None], wq, wo, gain_m[None], w_gate, w_up, w_down, turns(cache - 1, heads))
+        )(x, tall(k_cache), tall(v_cache), gain_a, wq, wo, gain_m, w_gate, w_up, w_down, turns(cache - 1, heads))
 
     states, cache, columns, rows_of = P("dp", None), P("dp", None, "tp", None), P(None, "tp"), P("tp", None)
     return jax.shard_map(

time: 81.4 us -> 73.2 us (0.90)
  Pallas kernels: 76.6 us -> 72.4 us
  local copies, waits for them, and re-layouts: 4.48 us -> 0.8 us
    pallas_call x1, Pallas kernels: 76.6 us -> 72.4 us  [step(): pl.pallas_call(functools.partial(layer_kernel, n, dims), out_shape=pltpu....]
    broadcast_in_dim x2 -> x0, local copies, waits for them, and re-layouts: 2.61 us -> none  [the longest x1 1.31 us: step(): gain_a[None]]
    unnamed x1, local copies, waits for them, and re-layouts: 1.87 us -> 0.8 us
where the time goes in v3:
time: 73.2 us
  Pallas kernels  72.4 us (99%)
  local copies, waits for them, and re-layouts  0.8 us (1%)
    pallas_call x1, Pallas kernels, step(): pl.pallas_call(functools.partial(layer_kernel, n, dims), out_shape=pltpu....  72.4 us

profile of v3, /device:TPU:96, one launch (start us, length us, event | category | flops | bytes accessed | tf_op | source)
XLA Modules:
  0.0 73.2 jit_solution(1738188789898406339)
XLA Ops:
  0.0 72.4 %layer.1 = bf16[64,4096]{1,0:T(8,128)(2,1)S(1)} custom-call(bf16[64,4096]{1,0:T(8,128)(2,1)} %x_hbm.1, bf16[64,256,2048]{2,1,0:T(8,128)(2,1)} %bitcast.1.k_hbm, bf16[64,256,2048]{2,1,0:T(8,128)(2,1)} %bitcast.3.v_hbm, bf16[4096]{0:T(1024)(128)(2,1)} %ga_hbm.1, bf16[4096,256]{1,0:T(8,128)(2,1)} %wq_hbm.1, bf16[256,4096]{1,0:T(8,128)(2,1)} %wo_hbm.1, ...), custom_call_target="tpu_custom_call" | custom-call | tf_op jit(solution)/shard_map/layer/pallas_call | solution.py:265
  72.4 0.8 %copy.13 = bf16[64,4096]{1,0:T(8,128)(2,1)} copy(bf16[64,4096]{1,0:T(8,128)(2,1)S(1)} %layer.1) | data formatting | bytes 1048576

commit v4 on v3

--- a/solution.py
+++ b/solution.py
@@ -16,6 +16,19 @@
 SLOTS = 3
 
 F32, BF16 = jnp.float32, jnp.bfloat16
+
+
+class Copies:
+    def __init__(self, parts):
+        self.parts = parts
+
+    def start(self):
+        for part in self.parts:
+            part.start()
+
+    def wait(self):
+        for part in self.parts:
+            part.wait()
 
 
 def iota(shape, axis):
@@ -58,7 +71,7 @@
 
     def take_k(g):
         s = lax.rem(g, SLOTS)
-        return pltpu.make_async_copy(k_hbm.at[pl.ds(g * GROUP, GROUP)], kbuf.at[s], k_sem.at[s])
+        return Copies([pltpu.make_async_copy(k_hbm.at[g * GROUP + b], kbuf.at[s, b], k_sem.at[s, b]) for b in range(GROUP)])
 
     def take_v(g, b):
         s = lax.rem(g, SLOTS)
@@ -73,12 +86,6 @@
         copy.start()
     take_wq.start()
     take_k(0).start()
-    for g in range(SLOTS):
-        if g + 1 < SLOTS:
-            take_k(g + 1).start()
-        start_v(g)
-        if g == 0:
-            take_wo.start()
 
     barrier = pltpu.get_barrier_semaphore()
     for k in range(1, n):
@@ -126,8 +133,15 @@
     for i, gain in enumerate((gain1, gain2)):
         gains[i : i + 1, :] = gain[...].astype(F32).reshape(1, width)
     take_x.wait()
+    take_k(1).start()
+    start_v(0)
     each(chunks, lambda c: norm(c, x, 0, a))
     take_wq.wait()
+    take_wo.start()
+    for g in range(1, SLOTS):
+        if g + 1 < SLOTS:
+            take_k(g + 1).start()
+        start_v(g)
     q = jnp.dot(a[...], wq[...], preferred_element_type=F32).astype(BF16).astype(F32)
     low = lax.rem(iota(q.shape, 1), HEAD) < HEAD // 2
     other = jnp.where(low, pltpu.roll(q, mine - HEAD // 2, 1), pltpu.roll(q, HEAD // 2, 1))
@@ -274,7 +288,7 @@
                 pltpu.VMEM((SLOTS, GROUP, mine, cache), BF16), pltpu.VMEM((SLOTS, GROUP, mine, cache), BF16),
                 pltpu.VMEM((GROUP * heads, cache), BF16), pltpu.VMEM((batch * heads, mine), BF16), pltpu.VMEM((CHUNK * heads, mine), BF16),
                 states, states, got, pltpu.VMEM((batch, hidden), BF16), states, got,
-                dma((9,)), dma((SLOTS,)), dma((SLOTS, GROUP)), dma, dma((chunks,)), dma((chunks,)), dma((chunks,)), dma((chunks,)),
+                dma((9,)), dma((SLOTS, GROUP)), dma((SLOTS, GROUP)), dma, dma((chunks,)), dma((chunks,)), dma((chunks,)), dma((chunks,)),
             ],
             compiler_params=pltpu.CompilerParams(collective_id=0, has_side_effects=True, vmem_limit_bytes=63 * 2**20),
             name="layer",

time: 73.2 us -> 73 us (level)
  no operation moved by 1% of the time
where the time goes in v4:
time: 73 us; the launch traced here: 72.9 us
  Pallas kernels  72.1 us (99%)
  local copies, waits for them, and re-layouts  0.8 us (1%)
    pallas_call x1, Pallas kernels, step(): pl.pallas_call(functools.partial(layer_kernel, n, dims), out_shape=pltpu....  72.1 us

profile of v4, /device:TPU:96, one launch (start us, length us, event | category | flops | bytes accessed | tf_op | source)
XLA Modules:
  0.0 72.9 jit_solution(5211986682561047075)
XLA Ops:
  0.0 72.1 %layer.1 = bf16[64,4096]{1,0:T(8,128)(2,1)S(1)} custom-call(bf16[64,4096]{1,0:T(8,128)(2,1)} %x_hbm.1, bf16[64,256,2048]{2,1,0:T(8,128)(2,1)} %bitcast.1.k_hbm, bf16[64,256,2048]{2,1,0:T(8,128)(2,1)} %bitcast.3.v_hbm, bf16[4096]{0:T(1024)(128)(2,1)} %ga_hbm.1, bf16[4096,256]{1,0:T(8,128)(2,1)} %wq_hbm.1, bf16[256,4096]{1,0:T(8,128)(2,1)} %wo_hbm.1, ...), custom_call_target="tpu_custom_call" | custom-call | tf_op jit(solution)/shard_map/layer/pallas_call | solution.py:279
  72.1 0.8 %copy.13 = bf16[64,4096]{1,0:T(8,128)(2,1)} copy(bf16[64,4096]{1,0:T(8,128)(2,1)S(1)} %layer.1) | data formatting | bytes 1048576
